TPU v7x, 128 devices: a whole 4x4x4 slice. The times are simulated.
128 devices in a mesh: owner: 8 (over x, core), rows: 16 (over z, y).
Axes of the slice: x: 4, y: 4, z: 4, core: 2. Of those that a mesh axis runs over, the one named last changes fastest.
Arguments:
- train_gate: float32 [128, 2048, 768], P('owner', 'rows'), may hold values from -0.1875 to 0.1875
- train_up: float32 [128, 2048, 768], P('owner', 'rows'), may hold values from -0.1875 to 0.1875
- router_weight: float32 [2048, 128], P('rows', 'owner'), may hold values from -0.125 to 0.125
- router_gain: float32 [2048], P('rows'), may hold values from 0.25 to 1.75
Outputs:
- ready_gate: bfloat16 [128, 2048, 768], P(('owner', 'rows'))
- ready_up: bfloat16 [128, 2048, 768], P(('owner', 'rows'))
- scale_gate: float32 [128, 768], P(('owner', 'rows'))
- scale_up: float32 [128, 768], P(('owner', 'rows'))
- serve_router: bfloat16 [2048, 128], replicated
All inputs are finite; a program needn't handle non-finite values.
Results may differ from a plain program's by a relative error of at most 0.001.
Values may be sent and summed in bfloat16 or wider, within the bound.
A program may use at most 128 MiB of HBM per device.

v0:
```python
import jax
import jax.numpy as jnp
from jax import lax
from jax.sharding import Mesh
from jax.sharding import PartitionSpec as P

OWNER = ("owner_0", "owner_1")
OWNER_ROWS = ("owner_0", "owner_1", "rows")


def from_everyone(value, axis):
    devices = lax.axis_size(axis)
    return lax.all_to_all(
        jnp.broadcast_to(value[None], (devices, *value.shape)), axis, 0, 0, tiled=True
    )


def taken_together(value, axis):
    return from_everyone(value, axis).sum(axis=0)


def in_one(arrays, axis):
    ends = [0]
    for a in arrays:
        ends.append(ends[-1] + a.size)
    total = taken_together(jnp.concatenate([a.ravel() for a in arrays]), axis)
    return tuple((total[b:e].reshape(a.shape) for a, b, e in zip(arrays, ends, ends[1:])))


def sent_together(arrays, axis, split_dim, concat_dim, along):
    both = jnp.concatenate(arrays, axis=along)
    out, at, done = (
        lax.all_to_all(both, axis, split_axis=split_dim, concat_axis=concat_dim, tiled=True),
        0,
        [],
    )
    for a in arrays:
        done.append(lax.slice_in_dim(out, at, at + a.shape[along], axis=along))
        at += a.shape[along]
    return tuple(done)


def laid_out(parts, dim):
    lengths = list(parts.shape[1:])
    lengths[dim] *= parts.shape[0]
    return jnp.moveaxis(parts, 0, dim).reshape(lengths)


def gathered_copies(value, axis, dim):
    return laid_out(from_everyone(value, axis), dim)


def stacked_from(value, axes, sequence):
    parts = value
    for k in sequence:
        parts = lax.all_gather(parts, axes[k])
    done = sequence[::-1]
    back = [done.index(k) for k in range(len(axes))]
    parts = parts.transpose(*back, *range(len(axes), parts.ndim))
    return parts.reshape(-1, *value.shape)


def whole_of(value, axes, sequence, dim):
    return laid_out(stacked_from(value, axes, sequence), dim)


def on_device(train_gate, train_up, router_weight, router_gain):
    total_gate, total_up = in_one(
        (jnp.sum(train_gate * train_gate, axis=1), jnp.sum(train_up * train_up, axis=1)), "rows"
    )
    scale_gate = jnp.sqrt(total_gate)
    scale_up = jnp.sqrt(total_up)
    narrow_gate, narrow_up = (
        (train_gate / jnp.expand_dims(scale_gate, 1)).astype(jnp.bfloat16),
        (train_up / jnp.expand_dims(scale_up, 1)).astype(jnp.bfloat16),
    )
    ready_gate, ready_up = sent_together((narrow_gate, narrow_up), "rows", 0, 1, 2)
    scale_gate = lax.dynamic_slice_in_dim(
        scale_gate, lax.axis_index("rows") * ready_gate.shape[0], ready_gate.shape[0], axis=0
    )
    scale_up = lax.dynamic_slice_in_dim(
        scale_up, lax.axis_index("rows") * ready_up.shape[0], ready_up.shape[0], axis=0
    )
    part_router = (router_weight * router_gain[:, None]).astype(jnp.bfloat16)
    row_router = gathered_copies(part_router, "rows", 0)
    serve_router = whole_of(row_router, ("owner_0", "owner_1"), (0, 1), 1)
    return (ready_gate, ready_up, scale_gate, scale_up, serve_router)


def solution(mesh):
    finer = Mesh(mesh.devices.reshape(4, 2, mesh.shape["rows"]), ("owner_0", "owner_1", "rows"))
    return jax.shard_map(
        on_device,
        mesh=finer,
        in_specs=(P(OWNER, "rows", None), P(OWNER, "rows", None), P("rows", OWNER), P("rows")),
        out_specs=(
            P(OWNER_ROWS, None, None),
            P(OWNER_ROWS, None, None),
            P(OWNER_ROWS, None),
            P(OWNER_ROWS, None),
            P(),
        ),
        check_vma=False,
    )
```

profile of v0, /device:TPU:0, one launch (start us, length us, event | category | flops | bytes accessed | tf_op | source)
XLA Modules:
  0.0 161.2 jit_solution(398515752994868322)
XLA Ops:
  0.6 3.3 %multiply_reduce_fusion.1 = f32[16,768]{1,0:T(8,128)S(1)} fusion(f32[16,128,768]{2,1,0:T(8,128)} %param.4), kind=kLoop, calls=%fused_computation.4 | loop fusion | flops 3133440 | bytes 6340608 | tf_op jit(solution)/shard_map/reduce_sum | solution.py:69
  4.0 0.0 copy-start
  4.0 0.0 copy-start.1
  4.0 3.3 %multiply_reduce_fusion = f32[16,768]{1,0:T(8,128)S(1)} fusion(f32[16,128,768]{2,1,0:T(8,128)} %param.5), kind=kLoop, calls=%fused_computation.3 | loop fusion | flops 3133440 | bytes 6340608 | tf_op jit(solution)/shard_map/reduce_sum | solution.py:69
  7.4 2.4 %broadcast_in_dim.4 = f32[16,1,24576]{2,1,0:T(1,128)} broadcast(f32[24576]{0:T(1024)S(1)} %pad_maximum_fusion.1), dimensions={2} | broadcast | bytes 1671168 | tf_op jit(solution)/shard_map/broadcast_in_dim | solution.py:14
  9.7 8.2 %all-to-all-start = ((f32[16,1,24576]{2,1,0:T(1,128)}), f32[16,1,24576]{2,1,0:T(1,128)S(1)}, u32[]{:S(2)}, u32[]{:S(2)}) async-start(f32[16,1,24576]{2,1,0:T(1,128)} %broadcast_in_dim.4), calls=%async_computation | async-start | bytes 3145728 | tf_op jit(solution)/shard_map/all_to_all | solution.py:13
  17.9 0.0 copy-done
  17.9 0.0 copy-done.1
  17.9 24.5 %all-to-all-done = f32[16,1,24576]{2,1,0:T(1,128)S(1)} async-done(((f32[16,1,24576]{2,1,0:T(1,128)}), f32[16,1,24576]{2,1,0:T(1,128)S(1)}, u32[]{:S(2)}, u32[]{:S(2)}) %all-to-all-start) | async-done | bytes 1572896 | tf_op jit(solution)/shard_map/all_to_all | solution.py:13
  42.4 0.6 broadcast_in_dim.5
  43.1 3.5 %all-to-all-start.2 = ((bf16[16,128,16]{1,2,0:T(8,128)(2,1)}), bf16[16,128,16]{1,2,0:T(8,128)(2,1)S(1)}, u32[]{:S(2)}, u32[]{:S(2)}) async-start(bf16[16,128,16]{1,2,0:T(8,128)(2,1)} %broadcast_in_dim.5), calls=%async_computation.2 | async-start | bytes 131072 | tf_op jit(solution)/shard_map/all_to_all | solution.py:13
  46.6 1.0 reduce_sum.29
  47.7 5.3 %divide_convert_fusion = (bf16[16,128,768]{2,1,0:T(8,128)(2,1)S(1)}, bf16[16,128,768]{2,1,0:T(8,128)(2,1)S(1)}) fusion(f32[16,128,768]{2,1,0:T(8,128)} %param.5, f32[16,768]{1,0:T(8,128)S(1)} %sqrt.15, f32[16,128,768]{2,1,0:T(8,128)} %param.4, f32[16,768]{1,0:T(8,128)S(1)} %sqrt.13), kind=kLoop, calls=%fused_computation.1 | loop fusion | flops 6291456 | bytes 18972672 | tf_op jit(solution)/shard_map/convert_element_type | solution.py:75
  53.0 3.2 %pad_maximum_fusion = bf16[16,128,1536]{2,1,0:T(8,128)(2,1)} fusion(bf16[16,128,768]{2,1,0:T(8,128)(2,1)S(1)} %get-tuple-element.39, bf16[16,128,768]{2,1,0:T(8,128)(2,1)S(1)} %get-tuple-element.40), kind=kLoop, calls=%fused_computation | loop fusion | flops 12582912 | bytes 12582912 | tf_op jit(solution)/shard_map/concatenate | solution.py:31
  56.2 0.0 all-to-all-done.2
  56.2 7.2 %all-to-all-start.1 = ((bf16[16,128,1536]{2,1,0:T(8,128)(2,1)}), bf16[16,128,1536]{2,1,0:T(8,128)(2,1)}, u32[]{:S(2)}, u32[]{:S(2)}) async-start(bf16[16,128,1536]{2,1,0:T(8,128)(2,1)} %pad_maximum_fusion), calls=%async_computation.1 | async-start | bytes 12582912 | tf_op jit(solution)/shard_map/all_to_all | solution.py:33
  63.5 12.7 %all_gather.9 = bf16[4,2048,16]{1,2,0:T(8,128)(2,1)S(1)} all-gather(bf16[1,2048,16]{1,2,0:T(8,128)(2,1)S(1)} %all_gather_reshape.3), channel_id=1, replica_groups=mesh['owner_0'=4,'owner_1'=2,'rows'=16] {'owner_0'}, dimensions={0}, use_global_device_ids=true | all-gather | bytes 327680 | tf_op jit(solution)/shard_map/all_gather | solution.py:56
  76.2 2.2 %all-gather = bf16[8,2048,16]{1,2,0:T(8,128)(2,1)S(1)} all-gather(bf16[4,2048,16]{1,2,0:T(8,128)(2,1)S(1)} %all_gather.9), channel_id=2, replica_groups=mesh['owner_0'=4,'owner_1'=2,'rows'=16] {'owner_1'}, dimensions={0}, use_global_device_ids=true | all-gather | bytes 786432 | tf_op jit(solution)/shard_map/all_gather | solution.py:56
  78.4 1.0 copy.24
  79.4 0.6 constant_dynamic-slice_fusion
  80.0 75.3 %all-to-all-done.1 = bf16[16,128,1536]{2,1,0:T(8,128)(2,1)} async-done(((bf16[16,128,1536]{2,1,0:T(8,128)(2,1)}), bf16[16,128,1536]{2,1,0:T(8,128)(2,1)}, u32[]{:S(2)}, u32[]{:S(2)}) %all-to-all-start.1) | async-done | bytes 6291488 | tf_op jit(solution)/shard_map/all_to_all | solution.py:33
  155.2 5.9 %fusion = (bf16[1,2048,768]{2,1,0:T(8,128)(2,1)}, bf16[1,2048,768]{2,1,0:T(8,128)(2,1)}) fusion(bf16[1,2048,1536]{2,1,0:T(8,128)(2,1)} %bitcast), kind=kLoop, calls=%fused_computation.11 | loop fusion | bytes 12582912 | tf_op jit(solution)/shard_map/slice | solution.py:38
  (10 shorter events, 0.2 us)
Async XLA Ops:
  4.0 13.9 %copy-start = (f32[128,16]{0,1:T(8,128)S(1)}, f32[128,16]{0,1:T(8,128)}, u32[]{:S(2)}) copy-start(f32[128,16]{0,1:T(8,128)} %param.6) | copy-start | bytes 24580
  4.0 13.9 %copy-start.1 = (f32[128]{0:T(128)S(1)}, f32[128]{0:T(128)}, u32[]{:S(2)}) copy-start(f32[128]{0:T(128)} %param.7) | copy-start | bytes 1540
  9.7 32.7 %all-to-all-start = ((f32[16,1,24576]{2,1,0:T(1,128)}), f32[16,1,24576]{2,1,0:T(1,128)S(1)}, u32[]{:S(2)}, u32[]{:S(2)}) async-start(f32[16,1,24576]{2,1,0:T(1,128)} %broadcast_in_dim.4), calls=%async_computation | async-start | bytes 3145728 | tf_op jit(solution)/shard_map/all_to_all | solution.py:13
  43.1 13.2 %all-to-all-start.2 = ((bf16[16,128,16]{1,2,0:T(8,128)(2,1)}), bf16[16,128,16]{1,2,0:T(8,128)(2,1)S(1)}, u32[]{:S(2)}, u32[]{:S(2)}) async-start(bf16[16,128,16]{1,2,0:T(8,128)(2,1)} %broadcast_in_dim.5), calls=%async_computation.2 | async-start | bytes 131072 | tf_op jit(solution)/shard_map/all_to_all | solution.py:13
  56.2 99.0 %all-to-all-start.1 = ((bf16[16,128,1536]{2,1,0:T(8,128)(2,1)}), bf16[16,128,1536]{2,1,0:T(8,128)(2,1)}, u32[]{:S(2)}, u32[]{:S(2)}) async-start(bf16[16,128,1536]{2,1,0:T(8,128)(2,1)} %pad_maximum_fusion), calls=%async_computation.1 | async-start | bytes 12582912 | tf_op jit(solution)/shard_map/all_to_all | solution.py:33
where the time goes:
time: 162 us; the launch traced here: 161 us
  waiting for transfers between devices  99.7 us (62%)
  starting transfers between devices  18.9 us (12%)
  other arithmetic  16.2 us (10%)
  blocking collectives  14.8 us (9%)
  local copies, waits for them, and re-layouts  10.7 us (7%)
    all_to_all x1, waiting for transfers between devices, sent_together(): lax.all_to_all(both, axis, split_axis=split_dim, concat_axis=concat_dim,...  75.3 us
    all_to_all x2, waiting for transfers between devices, from_everyone(): lax.all_to_all(jnp.broadcast_to(value[None], (devices, *value.shape)), ax...  24.5 us
    all_gather x2, blocking collectives, stacked_from(): parts = lax.all_gather(parts, axes[k])  14.8 us
    all_to_all x2, starting transfers between devices, from_everyone(): lax.all_to_all(jnp.broadcast_to(value[None], (devices, *value.shape)), ax...  11.7 us
    all_to_all x1, starting transfers between devices, sent_together(): lax.all_to_all(both, axis, split_axis=split_dim, concat_axis=concat_dim,...  7.2 us
    slice x1, local copies, waits for them, and re-layouts, sent_together(): done.append(lax.slice_in_dim(out, at, at + a.shape[along], axis=along))  5.95 us
    convert_element_type x1, other arithmetic, on_device(): (train_up / jnp.expand_dims(scale_up, 1)).astype(jnp.bfloat16)  5.31 us
    reduce_sum x1, other arithmetic, on_device(): jnp.sum(train_gate * train_gate, axis=1)  3.33 us
  transfers between devices with their start and end apart: 3, of which 2 were waited for; matrix products, arithmetic and copies ran while one was open for 7% of the time, Pallas kernels for 0%

commit v1 on v0

v1 whole, which is shorter than its diff:
```python
import functools

import jax
import jax.numpy as jnp
from jax import lax
from jax.experimental import pallas as pl
from jax.experimental.pallas import tpu as pltpu
from jax.sharding import PartitionSpec as P

MESH = pl.DeviceIdType.MESH
F32, BF16 = jnp.float32, jnp.bfloat16
SIDE = 4
ROWS = SIDE * SIDE
OWNERS = 8
LANES = 128
TILES = 6
EARLY = 2
LATE = TILES - EARLY
REST = LATE + TILES
PART = 2
GROUP = 4


def wrap(k):
    return lax.rem(k * 5, ROWS)


def exchange(
    gate, up, weight, gain,
    land, router, total,
    full, stage, early_y, early_z, late, late_in, late_all, early_total, inverse, late_inverse,
    weight_in, gain_in,
    load_sem, small_sem, y_send, y_recv, z_send, z_recv,
    sum_send, sum_recv, all_send, all_recv,
    data_send, data_recv, plane_send, plane_recv, owner_send, owner_recv,
):
    me = lax.axis_index("rows")
    own = lax.axis_index("owner")
    z, y = me // SIDE, lax.rem(me, SIDE)
    width = PART * LANES

    def rank(k):
        offset = wrap(k)
        to_z = lax.rem(z + offset // SIDE, SIDE)
        return to_z * SIDE + lax.rem(y + lax.rem(offset, SIDE), SIDE)

    def source(k):
        offset = wrap(k)
        from_z = lax.rem(z + SIDE - offset // SIDE, SIDE)
        return from_z * SIDE + lax.rem(y + SIDE - lax.rem(offset, SIDE), SIDE)

    def remote(src, dst, send, recv, **to):
        return pltpu.make_async_remote_copy(
            src_ref=src, dst_ref=dst, send_sem=send, recv_sem=recv,
            device_id=to, device_id_type=MESH,
        )

    loads = []
    early_width = EARLY * LANES
    late_width = LATE * LANES
    for matrix, ref, start, columns in (
        (0, gate, 0, early_width), (0, gate, early_width, late_width), (1, up, 0, TILES * LANES),
    ):
        here = []
        for g in range(ROWS // GROUP):
            part = (pl.ds(g * GROUP, GROUP), slice(None), pl.ds(start, columns))
            copy = pltpu.make_async_copy(
                ref.at[part], full.at[(matrix, *part)], load_sem.at[len(loads), g]
            )
            copy.start()
            here.append(copy)
        loads.append(here)
    weight_copy = pltpu.make_async_copy(weight, weight_in, small_sem.at[0])
    gain_copy = pltpu.make_async_copy(gain, gain_in, small_sem.at[1])
    weight_copy.start()
    gain_copy.start()

    barrier = pltpu.get_barrier_semaphore()
    for k in range(1, ROWS):
        pl.semaphore_signal(barrier, inc=1, device_id={"rows": lax.rem(me + k, ROWS)}, device_id_type=MESH)
    for k in range(1, OWNERS):
        pl.semaphore_signal(barrier, inc=1, device_id={"owner": lax.rem(own + k, OWNERS)}, device_id_type=MESH)

    def squares(matrix, e, tile):
        x = full[matrix, e, :, pl.ds(tile * LANES, LANES)]
        return jnp.sum(x * x, axis=0, keepdims=True)

    late[...] = jnp.zeros_like(late)
    for g in range(ROWS // GROUP):
        loads[0][g].wait()

        @pl.loop(g * GROUP, (g + 1) * GROUP)
        def _(e):
            for t in range(EARLY):
                early_y[y, pl.ds(e * EARLY + t, 1), :] = squares(0, e, t)

    pl.semaphore_wait(barrier, ROWS + OWNERS - 2)

    def across(slots, at, send, recv, axis):
        copies = []
        for d in range(1, SIDE):
            to = lax.rem(at + d, SIDE)
            peer = z * SIDE + to if axis == "y" else to * SIDE + y
            copies.append(remote(slots.at[at], slots.at[at], send.at[d], recv.at[d], rows=peer))
        for copy in copies:
            copy.start()
        return copies

    y_copies = across(early_y, y, y_send, y_recv, "y")

    for g in range(ROWS // GROUP):
        loads[1][g].wait()

        @pl.loop(g * GROUP, (g + 1) * GROUP)
        def _(e):
            for t in range(LATE):
                late[e, pl.ds(t, 1), :] = squares(0, e, EARLY + t)

    for g in range(ROWS // GROUP):
        loads[2][g].wait()

        @pl.loop(g * GROUP, (g + 1) * GROUP)
        def _(e):
            for t in range(TILES):
                late[e, pl.ds(LATE + t, 1), :] = squares(1, e, t)

    weight_copy.wait()
    gain_copy.wait()
    router[own, me] = (weight_in[...] * gain_in[...]).astype(BF16)

    for copy in y_copies:
        copy.wait_recv()
    early_z[z] = ((early_y[0] + early_y[1]) + early_y[2]) + early_y[3]
    z_copies = across(early_z, z, z_send, z_recv, "z")

    @pl.loop(1, ROWS)
    def _(k):
        remote(
            late.at[rank(k)], late_in.at[me], sum_send.at[k], sum_recv.at[k], rows=rank(k)
        ).start()

    late_in[me] = late[me]

    for copy in z_copies:
        copy.wait_recv()
    early = ((early_z[0] + early_z[1]) + early_z[2]) + early_z[3]
    early_total[...] = early
    inverse[...] = 1.0 / jnp.sqrt(early)

    def fill(part, e, write):
        matrix, start = part // (TILES // PART), (part % (TILES // PART)) * PART
        for t in range(PART):
            tile = start + t
            if matrix == 0 and tile < EARLY:
                row = inverse[pl.ds(e * EARLY + tile, 1), :]
            else:
                row = late_inverse[e, pl.ds(tile - EARLY if matrix == 0 else LATE + tile, 1), :]
            columns = pl.ds(tile * LANES, LANES)
            write(matrix, columns, (full[matrix, e, :, columns] * row).astype(BF16))

    def for_partner(k, part):
        to = rank(k)

        def write(matrix, columns, value):
            stage[to, pl.ds(matrix * LANES, LANES), columns] = value

        fill(part, to, write)

    def send(k, part):
        matrix, start = part // (TILES // PART), (part % (TILES // PART)) * width
        to = rank(k)
        piece = (pl.ds(matrix * LANES, LANES), pl.ds(start, width))
        remote(
            stage.at[(to, *piece)], land.at[(me, *piece)], data_send.at[k], data_recv.at[k], rows=to
        ).start()

    def batch(part, first, last):
        for_partner(first, part)

        @pl.loop(first + 1, last)
        def _(k):
            for_partner(k, part)
            send(k - 1, part)

        send(last - 1, part)

    def for_self(part):
        def write(matrix, columns, value):
            land[me, pl.ds(matrix * LANES, LANES), columns] = value

        fill(part, me, write)

    batch(0, 1, ROWS // 2)

    @pl.loop(1, ROWS)
    def _(k):
        remote(
            late.at[rank(k)], late_in.at[source(k)], sum_send.at[k], sum_recv.at[k], rows=rank(k)
        ).wait_recv()

    whole = late_in[0]
    for r in range(1, ROWS):
        whole = whole + late_in[r]
    late_all[me] = whole

    @pl.loop(1, ROWS)
    def _(k):
        remote(late_all.at[me], late_all.at[me], all_send.at[k], all_recv.at[k], rows=rank(k)).start()

    batch(0, ROWS // 2, ROWS)
    for_self(0)

    @pl.loop(1, ROWS)
    def _(k):
        remote(
            router.at[own, me], router.at[own, me], plane_send.at[k], plane_recv.at[k], rows=rank(k)
        ).start()

    for t in range(EARLY):
        total[t] = early_total[pl.ds(me * EARLY + t, 1), :]
    for t in range(REST):
        total[EARLY + t] = late_all[me, pl.ds(t, 1), :]

    @pl.loop(1, ROWS)
    def _(k):
        remote(
            late_all.at[me], late_all.at[source(k)], all_send.at[k], all_recv.at[k], rows=rank(k)
        ).wait_recv()

    late_inverse[...] = 1.0 / jnp.sqrt(late_all[...])

    for part in range(1, 2 * TILES // PART):
        batch(part, 1, ROWS)
        for_self(part)
        if part == 1:
            @pl.loop(1, ROWS)
            def _(k):
                remote(
                    router.at[own, me], router.at[own, source(k)], plane_send.at[k], plane_recv.at[k], rows=rank(k)
                ).wait_recv()

            for k in range(1, OWNERS):
                remote(
                    router.at[own], router.at[own], owner_send.at[k], owner_recv.at[k],
                    owner=lax.rem(own + k, OWNERS),
                ).start()

    for copy in y_copies + z_copies:
        copy.wait_send()

    @pl.loop(1, ROWS)
    def _(k):
        to = rank(k)
        remote(late.at[to], late_in.at[me], sum_send.at[k], sum_recv.at[k], rows=to).wait_send()
        remote(late_all.at[me], late_all.at[me], all_send.at[k], all_recv.at[k], rows=to).wait_send()
        remote(router.at[own, me], router.at[own, me], plane_send.at[k], plane_recv.at[k], rows=to).wait_send()

    for k in range(1, OWNERS):
        copy = remote(
            router.at[own], router.at[lax.rem(own + OWNERS - k, OWNERS)], owner_send.at[k], owner_recv.at[k],
            owner=lax.rem(own + k, OWNERS),
        )
        copy.wait_send()
        copy.wait_recv()

    @pl.loop(1, ROWS)
    def _(k):
        copy = remote(stage.at[rank(k)], land.at[source(k)], data_send.at[k], data_recv.at[k], rows=rank(k))
        copy.wait_send()
        copy.wait_recv()


def lay_out(land, router, total, gate, up, scale_gate, scale_up, serve, sem):
    copies = []
    for half in range(2):
        for matrix, out in ((0, gate), (1, up)):
            some = pl.ds(half * ROWS // 2, ROWS // 2)
            copy = pltpu.make_async_copy(
                land.at[some, pl.ds(matrix * LANES, LANES)], out.at[some], sem.at[half, matrix]
            )
            copy.start()
            copies.append(copy)
    for t in range(TILES):
        columns = slice(t * LANES, (t + 1) * LANES)
        scale_gate[:, columns] = jnp.sqrt(total[t])
        scale_up[:, columns] = jnp.sqrt(total[TILES + t])
    for r in range(ROWS):
        block = jnp.concatenate([router[o, r] for o in range(OWNERS)], axis=0).astype(F32)
        serve[r * LANES:(r + 1) * LANES, :] = block.T.astype(BF16)
    for copy in copies:
        copy.wait()


def on_device(gate, up, weight, gain):
    hbm = pl.BlockSpec(memory_space=pltpu.HBM)
    vmem = pl.BlockSpec(memory_space=pltpu.VMEM)
    experts, rows, columns = gate.shape
    dma = pltpu.SemaphoreType.DMA
    land, router, total = pl.pallas_call(
        exchange,
        name="exchange",
        out_shape=(
            jax.ShapeDtypeStruct((ROWS, 2 * rows, columns), BF16),
            jax.ShapeDtypeStruct((OWNERS, ROWS, LANES // OWNERS, rows), BF16),
            jax.ShapeDtypeStruct((2 * TILES, 1, LANES), F32),
        ),
        in_specs=[hbm] * 4,
        out_specs=(vmem,) * 3,
        scratch_shapes=[
            pltpu.VMEM((2, experts, rows, columns), F32),
            pltpu.VMEM((ROWS, 2 * rows, columns), BF16),
            pltpu.VMEM((SIDE, experts * EARLY, LANES), F32),
            pltpu.VMEM((SIDE, experts * EARLY, LANES), F32),
            pltpu.VMEM((experts, 16, LANES), F32),
            pltpu.VMEM((experts, 16, LANES), F32),
            pltpu.VMEM((experts, 16, LANES), F32),
            pltpu.VMEM((experts * EARLY, LANES), F32),
            pltpu.VMEM((experts * EARLY, LANES), F32),
            pltpu.VMEM((experts, 16, LANES), F32),
            pltpu.VMEM((LANES // OWNERS, rows), F32),
            pltpu.VMEM((1, rows), F32),
            dma((3, ROWS // GROUP)),
            dma((2,)),
            dma((SIDE,)), dma((SIDE,)), dma((SIDE,)), dma((SIDE,)),
            dma((ROWS,)), dma((ROWS,)), dma((ROWS,)), dma((ROWS,)),
            dma((ROWS,)), dma((ROWS,)), dma((ROWS,)), dma((ROWS,)),
            dma((OWNERS,)), dma((OWNERS,)),
        ],
        compiler_params=pltpu.CompilerParams(
            collective_id=0, has_side_effects=True, vmem_limit_bytes=36 << 20
        ),
    )(*(pltpu.with_memory_space_constraint(a, pltpu.HBM) for a in (gate, up, weight.T, gain.reshape(1, rows))))
    ready = jax.ShapeDtypeStruct((ROWS, rows, columns), BF16)
    scale = jax.ShapeDtypeStruct((1, columns), F32)
    ready_gate, ready_up, scale_gate, scale_up, serve = pl.pallas_call(
        lay_out,
        name="lay_out",
        out_shape=(ready, ready, scale, scale, jax.ShapeDtypeStruct((ROWS * rows, LANES), BF16)),
        in_specs=[vmem] * 3,
        out_specs=(hbm, hbm, vmem, vmem, vmem),
        scratch_shapes=[dma((2, 2))],
        compiler_params=pltpu.CompilerParams(vmem_limit_bytes=16 << 20),
    )(land, router, total)
    whole = (1, ROWS * rows, columns)
    return ready_gate.reshape(whole), ready_up.reshape(whole), scale_gate, scale_up, serve


def solution(mesh):
    return jax.shard_map(
        on_device,
        mesh=mesh,
        in_specs=(P("owner", "rows", None), P("owner", "rows", None), P("rows", "owner"), P("rows")),
        out_specs=(
            P(("owner", "rows"), None, None),
            P(("owner", "rows"), None, None),
            P(("owner", "rows"), None),
            P(("owner", "rows"), None),
            P(),
        ),
        check_vma=False,
    )
```

time: 162 us -> 92.2 us (0.57)
  waiting for transfers between devices: 99.7 us -> 0 us
  Pallas kernels: 0 us -> 91.4 us
  starting transfers between devices: 18.9 us -> 0 us
  other arithmetic: 16.2 us -> 0 us
  blocking collectives: 14.8 us -> 0 us
  local copies, waits for them, and re-layouts: 10.7 us -> 0 us
    all_to_all x3 -> x0, waiting for transfers between devices: 99.7 us -> none  [the longest x1 75.3 us: sent_together(): lax.all_to_all(both, axis, split_axis=split_dim, concat_axis=concat_dim,...]
    pallas_call x0 -> x2, Pallas kernels: none -> 91.4 us  [the longest x1 87.8 us: on_device(): pl.pallas_call(exchange, name='exchange', out_shape=(jax.ShapeDtypeStruct...]
    all_to_all x3 -> x0, starting transfers between devices: 18.9 us -> none  [the longest x2 11.7 us: from_everyone(): lax.all_to_all(jnp.broadcast_to(value[None], (devices, *value.shape)), ax...]
    all_gather x2 -> x0, blocking collectives: 14.8 us -> none  [stacked_from(): parts = lax.all_gather(parts, axes[k])]
    reduce_sum x3 -> x0, other arithmetic: 7.69 us -> none  [the longest x1 3.33 us: on_device(): jnp.sum(train_gate * train_gate, axis=1)]
    slice x1 -> x0, local copies, waits for them, and re-layouts: 5.95 us -> none  [sent_together(): done.append(lax.slice_in_dim(out, at, at + a.shape[along], axis=along))]
    convert_element_type x2 -> x0, other arithmetic: 5.31 us -> none  [the longest x1 5.31 us: on_device(): (train_up / jnp.expand_dims(scale_up, 1)).astype(jnp.bfloat16)]
    concatenate x2 -> x0, other arithmetic: 3.23 us -> none  [the longest x1 3.22 us: sent_together(): both = jnp.concatenate(arrays, axis=along)]
  transfers between devices with their start and end apart: 3 -> 0, of which waited for: 2 -> 0; matrix products, arithmetic and copies ran while one was open for 7% -> 0% of each run, Pallas kernels for 0% -> 0%
where the time goes in v1:
time: 92.2 us; the launch traced here: 92 us
  Pallas kernels  91.4 us (99%)
    pallas_call x1, Pallas kernels, on_device(): pl.pallas_call(exchange, name='exchange', out_shape=(jax.ShapeDtypeStruct...  87.8 us
    pallas_call x1, Pallas kernels, on_device(): pl.pallas_call(lay_out, name='lay_out', out_shape=(ready, ready, scale, s...  3.6 us

profile of v1, /device:TPU:0, one launch (start us, length us, event | category | flops | bytes accessed | tf_op | source)
XLA Modules:
  0.0 92.0 jit_solution(13612937727057934271)
XLA Ops:
  0.6 87.8 %exchange.1 = (bf16[16,256,768]{2,1,0:T(8,128)(2,1)S(1)}, bf16[8,16,16,128]{3,2,1,0:T(8,128)(2,1)S(1)}, f32[12,1,128]{2,1,0:T(1,128)S(1)}) custom-call(f32[16,128,768]{2,1,0:T(8,128)} %gate.1, f32[16,128,768]{2,1,0:T(8,128)} %up.1, f32[16,128]{1,0:T(8,128)} %bitcast.4, f32[1,128]{1,0:T(1,128)} %bitcast.5), custom_call_target="tpu_custom_call" | custom-call | tf_op jit(solution)/shard_map/exchange/pallas_call | solution.py:299
  88.4 3.6 %lay_out.1 = (bf16[16,128,768]{2,1,0:T(8,128)(2,1)}, bf16[16,128,768]{2,1,0:T(8,128)(2,1)}, f32[1,768]{1,0:T(1,128)}, f32[1,768]{1,0:T(1,128)}, bf16[2048,128]{1,0:T(8,128)(2,1)}) custom-call(bf16[16,256,768]{2,1,0:T(8,128)(2,1)S(1)} %get-tuple-element.13.land, bf16[8,16,16,128]{3,2,1,0:T(8,128)(2,1)S(1)} %get-tuple-element.14.router, ...), custom_call_target="tpu_custom_call" | custom-call | tf_op jit(solution)/shard_map/lay_out/pallas_call | solution.py:335

commit v2 on v0

v2 whole, which is shorter than its diff:
```python
import jax
import jax.numpy as jnp
from jax import lax
from jax.experimental import pallas as pl
from jax.experimental.pallas import tpu as pltpu
from jax.sharding import PartitionSpec as P

MESH = pl.DeviceIdType.MESH
F32, BF16 = jnp.float32, jnp.bfloat16
SIDE = 4
ROWS = SIDE * SIDE
OWNERS = 8
LANES = 128
DEEP = 128
TILES = 6
PART = 2
PARTS = TILES // PART
FIRST = 2
EARLY = FIRST * PART
LATE = 2 * TILES - EARLY
GROUP = 4
RAW = 32
HALF = RAW // 2
ORDER = (
    (2, 2), (3, 2), (2, 3), (1, 2), (2, 1), (2, 0), (0, 2), (3, 1), (1, 3), (3, 3), (1, 1), (1, 0), (0, 3), (3, 0), (0, 1),
)
NEAR = tuple(step for step in ORDER if 0 in step)


def exchange(
    gate, up, weight, gain,
    land, serve, scale_gate, scale_up,
    full, stage, raw, router, early_y, early_z, early_total,
    late, late_y, late_sum, late_z, late_all, inverse, weight_in, gain_in,
    load_sem, small_sem, y_send, y_recv, z_send, z_recv, raw_send, raw_recv,
    late_y_send, late_y_recv, late_z_send, late_z_recv, all_send, all_recv,
    data_send, data_recv, plane_send, plane_recv, owner_send, owner_recv,
):
    me = lax.axis_index("rows")
    own = lax.axis_index("owner")
    z, y = me // SIDE, lax.rem(me, SIDE)
    width = PART * LANES

    def shifted(step):
        return lax.rem(z + step[0], SIDE) * SIDE + lax.rem(y + step[1], SIDE)

    def back(step):
        return shifted((SIDE - step[0], SIDE - step[1]))

    def slot(step):
        return step[0] * SIDE + step[1]

    def remote(src, dst, send, recv, **to):
        return pltpu.make_async_remote_copy(
            src_ref=src, dst_ref=dst, send_sem=send, recv_sem=recv,
            device_id=to, device_id_type=MESH,
        )

    loads = []
    for matrix, ref, start, tiles in (
        (0, gate, 0, PART), (0, gate, PART, EARLY - PART), (0, gate, EARLY, TILES - EARLY), (1, up, 0, TILES),
    ):
        here = []
        for g in range(ROWS // GROUP):
            part = (pl.ds(g * GROUP, GROUP), slice(None), pl.ds(start * LANES, tiles * LANES))
            copy = pltpu.make_async_copy(
                ref.at[part], full.at[(matrix, *part)], load_sem.at[len(loads), g]
            )
            copy.start()
            here.append(copy)
        loads.append(here)
    weight_copy = pltpu.make_async_copy(weight, weight_in, small_sem.at[0])
    gain_copy = pltpu.make_async_copy(gain, gain_in, small_sem.at[1])
    weight_copy.start()
    gain_copy.start()

    barrier = pltpu.get_barrier_semaphore()
    for step in NEAR:
        pl.semaphore_signal(barrier, inc=1, device_id={"rows": shifted(step)}, device_id_type=MESH)
    for d in range(1, OWNERS):
        pl.semaphore_signal(barrier, inc=1, device_id={"owner": lax.rem(own + d, OWNERS)}, device_id_type=MESH)

    def squares(matrix, e, tile):
        x = full[matrix, e, :, pl.ds(tile * LANES, LANES)]
        return jnp.sum(x * x, axis=0, keepdims=True)

    def early_squares(i):
        for g in range(ROWS // GROUP):
            loads[i][g].wait()

            @pl.loop(g * GROUP, (g + 1) * GROUP)
            def _(e):
                for t in range(PART):
                    early_y[i, y, e, t] = squares(0, e, i * PART + t)

    early_squares(0)
    pl.semaphore_wait(barrier, len(NEAR) + OWNERS - 1)

    def across(source, slots, at, send, recv, along_z):
        copies = []
        for d in (2, 1, 3):
            to = lax.rem((z if along_z else y) + d, SIDE)
            peer = shifted((d, 0) if along_z else (0, d))
            copies.append(remote(source(to), slots.at[at], send.at[d], recv.at[d], rows=peer))
            copies[-1].start()
        return copies

    def raw_copy(i, half):
        to = shifted(NEAR[i])
        return remote(
            up.at[to, pl.ds(DEEP - RAW + half * HALF, HALF)], raw.at[i, pl.ds(half * HALF, HALF)],
            raw_send.at[i, half], raw_recv.at[i, half], rows=to,
        )

    def early_across(i, slots, at, send, recv, along_z):
        return across(lambda to: slots.at[i, at], slots.at[i], at, send.at[i], recv.at[i], along_z)

    def taken(slots):
        return ((slots[0] + slots[1]) + slots[2]) + slots[3]

    y_copies = [early_across(0, early_y, y, y_send, y_recv, False)]
    if RAW:
        for i in range(len(NEAR)):
            raw_copy(i, 0).start()

    def late_squares(matrix, start, loaded):
        for g in range(ROWS // GROUP):
            loaded[g].wait()

            @pl.loop(g * GROUP, (g + 1) * GROUP)
            def _(e):
                for t in range(start, TILES):
                    late[lax.rem(e, SIDE), e // SIDE, matrix * TILES + t - EARLY] = squares(matrix, e, t)

    for i in range(1, FIRST):
        early_squares(i)
        y_copies.append(early_across(i, early_y, y, y_send, y_recv, False))
    late_squares(0, EARLY, loads[2])
    late_squares(1, 0, loads[3])
    late_y_copies = across(lambda to: late.at[to], late_y, y, late_y_send, late_y_recv, False)

    weight_copy.wait()
    gain_copy.wait()
    router[own, me] = (weight_in[...] * gain_in[...]).astype(BF16)
    late_y[y] = late[y]

    z_copies = []
    for i in range(FIRST):
        for copy in y_copies[i]:
            copy.wait_recv()
        early_z[i, z] = taken(early_y.at[i])
        z_copies.append(early_across(i, early_z, z, z_send, z_recv, True))
        if RAW and i == 0:
            for j in range(len(NEAR)):
                raw_copy(j, 1).start()

    for copy in late_y_copies:
        copy.wait_recv()
    late_sum[...] = taken(late_y)
    late_z[z] = late_sum[z]
    late_z_copies = across(lambda to: late_sum.at[to], late_z, z, late_z_send, late_z_recv, True)

    def early_whole(i):
        for copy in z_copies[i]:
            copy.wait_recv()
        whole = taken(early_z.at[i])
        early_total[:, i * PART:(i + 1) * PART] = whole
        inverse[:, i * PART:(i + 1) * PART] = 1.0 / jnp.sqrt(whole)

    def fill(part, e, deep, write):
        matrix, start = part // PARTS, lax.rem(part, PARTS) * PART
        for t in range(PART):
            columns = pl.ds(pl.multiple_of((start + t) * LANES, LANES), LANES)
            row = inverse[e, part * PART + t]
            value = (full[matrix, e, pl.ds(0, deep), columns] * row).astype(BF16)
            write(pl.ds(pl.multiple_of(matrix * DEEP, DEEP), deep), columns, value)

    def prepare(step, part, deep):
        to = shifted(step)

        def write(rows, columns, value):
            stage[to, rows, columns] = value

        fill(part, to, deep, write)

    def send(step, part, deep):
        piece = (
            pl.ds(pl.multiple_of(part // PARTS * DEEP, DEEP), deep),
            pl.ds(pl.multiple_of(lax.rem(part, PARTS) * width, width), width),
        )
        k = slot(step)
        to = shifted(step)
        remote(
            stage.at[(to, *piece)], land.at[(me, *piece)], data_send.at[k], data_recv.at[k], rows=to
        ).start()

    def batch(part, steps, less=0):
        waiting = None
        for step in steps:
            deep = DEEP - (less if step in NEAR else 0)
            prepare(step, part, deep)
            if waiting:
                send(waiting[0], part, waiting[1])
            waiting = step, deep
        send(waiting[0], part, waiting[1])

    def for_self(part):
        def write(rows, columns, value):
            land[me, rows, columns] = value

        fill(part, me, DEEP, write)

    early_whole(0)
    batch(0, ORDER)

    for copy in late_z_copies:
        copy.wait_recv()
    late_all[me] = taken(late_z)

    def all_copy(step, at):
        return remote(
            late_all.at[me], late_all.at[at], all_send.at[slot(step)], all_recv.at[slot(step)], rows=shifted(step)
        )

    for_self(0)
    for step in ORDER:
        all_copy(step, me).start()

    for part in range(1, FIRST):
        early_whole(part)
        batch(part, ORDER)

    def plane_copy(step, at):
        return remote(
            router.at[own, me], router.at[own, at], plane_send.at[slot(step)], plane_recv.at[slot(step)],
            rows=shifted(step),
        )

    for step in ORDER:
        plane_copy(step, me).start()

    for t in range(TILES):
        columns = pl.ds(t * LANES, LANES)
        scale_gate[:, columns] = jnp.sqrt(early_total[me, t] if t < EARLY else late_all[me, t - EARLY])
        scale_up[:, columns] = jnp.sqrt(late_all[me, TILES + t - EARLY])

    for step in ORDER:
        all_copy(step, back(step)).wait_recv()
    inverse[:, EARLY:] = 1.0 / jnp.sqrt(late_all[...])

    for part in range(FIRST, PARTS):
        batch(part, ORDER)

    @pl.loop(PARTS, 2 * PARTS)
    def _(part):
        batch(part, ORDER, RAW)

    @pl.loop(1, 2 * PARTS)
    def _(part):
        for_self(part)

    for step in ORDER:
        plane_copy(step, back(step)).wait_recv()

    def owner_copy(d, at):
        return remote(
            router.at[own], router.at[at], owner_send.at[d], owner_recv.at[d], owner=lax.rem(own + d, OWNERS)
        )

    for d in range(1, OWNERS):
        owner_copy(d, own).start()

    if RAW:
        for i, step in enumerate(NEAR):
            for half in range(2):
                raw_copy(i, half).wait_recv()
            for t in range(TILES):
                columns = pl.ds(t * LANES, LANES)
                land[back(step), pl.ds(2 * DEEP - RAW, RAW), columns] = (
                    raw[i, :, columns] * inverse[me, TILES + t]
                ).astype(BF16)

    for d in range(1, OWNERS):
        owner_copy(d, lax.rem(own + OWNERS - d, OWNERS)).wait_recv()
    for r in range(ROWS):
        block = jnp.concatenate([router[o, r] for o in range(OWNERS)], axis=0).astype(F32)
        serve[r * DEEP:(r + 1) * DEEP, :] = block.T.astype(BF16)

    for copy in sum(y_copies + z_copies, []) + late_y_copies + late_z_copies:
        copy.wait_send()
    if RAW:
        for i in range(len(NEAR)):
            for half in range(2):
                raw_copy(i, half).wait_send()
    for d in range(1, OWNERS):
        owner_copy(d, own).wait_send()
    for step in ORDER:
        all_copy(step, me).wait_send()
        plane_copy(step, me).wait_send()
    for step in ORDER:
        rows = pl.ds(0, 2 * DEEP - (RAW if step in NEAR else 0))
        k = slot(step)
        copy = remote(
            stage.at[shifted(step), rows], land.at[back(step), rows], data_send.at[k], data_recv.at[k],
            rows=shifted(step),
        )
        copy.wait_send()
        copy.wait_recv()


def lay_out(land, serve, scale_gate, scale_up, gate_out, up_out, serve_out, scale_gate_out, scale_up_out, sem):
    copies = [
        (land.at[:, pl.ds(0, DEEP)], gate_out),
        (land.at[:, pl.ds(DEEP, DEEP)], up_out),
        (serve, serve_out),
        (scale_gate, scale_gate_out),
        (scale_up, scale_up_out),
    ]
    copies = [pltpu.make_async_copy(src, dst, sem.at[i]) for i, (src, dst) in enumerate(copies)]
    for copy in copies:
        copy.start()
    for copy in copies:
        copy.wait()


def on_device(gate, up, weight, gain):
    hbm = pl.BlockSpec(memory_space=pltpu.HBM)
    vmem = pl.BlockSpec(memory_space=pltpu.VMEM)
    experts, rows, columns = gate.shape
    dma = pltpu.SemaphoreType.DMA
    scale = jax.ShapeDtypeStruct((1, columns), F32)
    router = jax.ShapeDtypeStruct((ROWS * rows, LANES), BF16)
    inputs = (gate, up, weight.T, gain.reshape(1, rows))
    sums = lambda *lead: pltpu.VMEM((*lead, 1, LANES), F32)
    done = pl.pallas_call(
        exchange,
        name="exchange",
        out_shape=(jax.ShapeDtypeStruct((ROWS, 2 * rows, columns), BF16), router, scale, scale),
        in_specs=[hbm] * 4,
        out_specs=(vmem,) * 4,
        scratch_shapes=[
            pltpu.VMEM((2, experts, rows, columns), F32),
            pltpu.VMEM((ROWS, 2 * rows, columns), BF16),
            pltpu.VMEM((len(NEAR), max(RAW, 8), columns), F32),
            pltpu.VMEM((OWNERS, ROWS, LANES // OWNERS, rows), BF16),
            sums(FIRST, SIDE, experts, PART),
            sums(FIRST, SIDE, experts, PART),
            sums(experts, EARLY),
            sums(SIDE, SIDE, LATE),
            sums(SIDE, SIDE, LATE),
            sums(SIDE, LATE),
            sums(SIDE, LATE),
            sums(experts, LATE),
            sums(experts, 2 * TILES),
            pltpu.VMEM((LANES // OWNERS, rows), F32),
            pltpu.VMEM((1, rows), F32),
            dma((4, ROWS // GROUP)),
            dma((2,)),
            dma((FIRST, SIDE)), dma((FIRST, SIDE)), dma((FIRST, SIDE)), dma((FIRST, SIDE)),
            dma((len(NEAR), 2)), dma((len(NEAR), 2)),
            dma((SIDE,)), dma((SIDE,)), dma((SIDE,)), dma((SIDE,)),
            dma((ROWS,)), dma((ROWS,)), dma((ROWS,)), dma((ROWS,)),
            dma((ROWS,)), dma((ROWS,)),
            dma((OWNERS,)), dma((OWNERS,)),
        ],
        compiler_params=pltpu.CompilerParams(
            collective_id=0, has_side_effects=True, vmem_limit_bytes=36 << 20
        ),
    )(*(pltpu.with_memory_space_constraint(a, pltpu.HBM) for a in inputs))
    ready = jax.ShapeDtypeStruct((ROWS, rows, columns), BF16)
    ready_gate, ready_up, serve, scale_gate, scale_up = pl.pallas_call(
        lay_out,
        name="lay_out",
        out_shape=(ready, ready, router, scale, scale),
        in_specs=[vmem] * 4,
        out_specs=(hbm,) * 5,
        scratch_shapes=[dma((5,))],
        compiler_params=pltpu.CompilerParams(vmem_limit_bytes=8 << 20),
    )(*done)
    whole = (1, ROWS * rows, columns)
    return ready_gate.reshape(whole), ready_up.reshape(whole), scale_gate, scale_up, serve


def solution(mesh):
    return jax.shard_map(
        on_device,
        mesh=mesh,
        in_specs=(P("owner", "rows", None), P("owner", "rows", None), P("rows", "owner"), P("rows")),
        out_specs=(
            P(("owner", "rows"), None, None),
            P(("owner", "rows"), None, None),
            P(("owner", "rows"), None),
            P(("owner", "rows"), None),
            P(),
        ),
        check_vma=False,
    )
```

time: 162 us -> 89.1 us (0.55)
  waiting for transfers between devices: 99.7 us -> 0 us
  Pallas kernels: 0 us -> 88.3 us
  starting transfers between devices: 18.9 us -> 0 us
  other arithmetic: 16.2 us -> 0 us
  blocking collectives: 14.8 us -> 0 us
  local copies, waits for them, and re-layouts: 10.7 us -> 0 us
    all_to_all x3 -> x0, waiting for transfers between devices: 99.7 us -> none  [the longest x1 75.3 us: sent_together(): lax.all_to_all(both, axis, split_axis=split_dim, concat_axis=concat_dim,...]
    pallas_call x0 -> x2, Pallas kernels: none -> 88.3 us  [the longest x1 85.4 us: on_device(): pl.pallas_call(exchange, name='exchange', out_shape=(jax.ShapeDtypeStruct...]
    all_to_all x3 -> x0, starting transfers between devices: 18.9 us -> none  [the longest x2 11.7 us: from_everyone(): lax.all_to_all(jnp.broadcast_to(value[None], (devices, *value.shape)), ax...]
    all_gather x2 -> x0, blocking collectives: 14.8 us -> none  [stacked_from(): parts = lax.all_gather(parts, axes[k])]
    reduce_sum x3 -> x0, other arithmetic: 7.69 us -> none  [the longest x1 3.33 us: on_device(): jnp.sum(train_gate * train_gate, axis=1)]
    slice x1 -> x0, local copies, waits for them, and re-layouts: 5.95 us -> none  [sent_together(): done.append(lax.slice_in_dim(out, at, at + a.shape[along], axis=along))]
    convert_element_type x2 -> x0, other arithmetic: 5.31 us -> none  [the longest x1 5.31 us: on_device(): (train_up / jnp.expand_dims(scale_up, 1)).astype(jnp.bfloat16)]
    concatenate x2 -> x0, other arithmetic: 3.23 us -> none  [the longest x1 3.22 us: sent_together(): both = jnp.concatenate(arrays, axis=along)]
  transfers between devices with their start and end apart: 3 -> 0, of which waited for: 2 -> 0; matrix products, arithmetic and copies ran while one was open for 7% -> 0% of each run, Pallas kernels for 0% -> 0%
where the time goes in v2:
time: 89.1 us; the launch traced here: 89 us
  Pallas kernels  88.3 us (99%)
    pallas_call x1, Pallas kernels, on_device(): pl.pallas_call(exchange, name='exchange', out_shape=(jax.ShapeDtypeStruct...  85.4 us
    pallas_call x1, Pallas kernels, on_device(): pl.pallas_call(lay_out, name='lay_out', out_shape=(ready, ready, router,...  2.91 us

profile of v2, /device:TPU:0, one launch (start us, length us, event | category | flops | bytes accessed | tf_op | source)
XLA Modules:
  0.0 89.0 jit_solution(16823928423066731061)
XLA Ops:
  0.6 85.4 %exchange.1 = (bf16[16,256,768]{2,1,0:T(8,128)(2,1)S(1)}, bf16[2048,128]{1,0:T(8,128)(2,1)S(1)}, f32[1,768]{1,0:T(1,128)S(1)}, f32[1,768]{1,0:T(1,128)S(1)}) custom-call(f32[16,128,768]{2,1,0:T(8,128)} %gate.1, f32[16,128,768]{2,1,0:T(8,128)} %up.1, f32[16,128]{1,0:T(8,128)} %bitcast.4, f32[1,128]{1,0:T(1,128)} %bitcast.5), custom_call_target="tpu_custom_call" | custom-call | tf_op jit(solution)/shard_map/exchange/pallas_call | solution.py:335
  86.1 2.9 %lay_out.1 = (bf16[16,128,768]{2,1,0:T(8,128)(2,1)}, bf16[16,128,768]{2,1,0:T(8,128)(2,1)}, bf16[2048,128]{1,0:T(8,128)(2,1)}, f32[1,768]{1,0:T(1,128)}, f32[1,768]{1,0:T(1,128)}) custom-call(bf16[16,256,768]{2,1,0:T(8,128)(2,1)S(1)} %get-tuple-element.14.land, bf16[2048,128]{1,0:T(8,128)(2,1)S(1)} %get-tuple-element.15.serve, ...), custom_call_target="tpu_custom_call" | custom-call | tf_op jit(solution)/shard_map/lay_out/pallas_call | solution.py:371

commit v3 on v2

--- a/solution.py
+++ b/solution.py
@@ -14,15 +14,14 @@
 DEEP = 128
 TILES = 6
 PART = 2
-PARTS = TILES // PART
-FIRST = 2
-EARLY = FIRST * PART
+EAGER = ((0, 1), (1, 2))
+EARLY = 3
 LATE = 2 * TILES - EARLY
 GROUP = 4
-RAW = 32
-HALF = RAW // 2
+RAW = 24
+HALF = 16
 ORDER = (
-    (2, 2), (3, 2), (2, 3), (1, 2), (2, 1), (2, 0), (0, 2), (3, 1), (1, 3), (3, 3), (1, 1), (1, 0), (0, 3), (3, 0), (0, 1),
+    (1, 2), (2, 3), (2, 0), (3, 1), (2, 1), (0, 2), (3, 3), (1, 1), (2, 2), (3, 2), (1, 3), (0, 3), (1, 0), (3, 0), (0, 1),
 )
 NEAR = tuple(step for step in ORDER if 0 in step)
 
@@ -30,7 +29,7 @@
 def exchange(
     gate, up, weight, gain,
     land, serve, scale_gate, scale_up,
-    full, stage, raw, router, early_y, early_z, early_total,
+    full, stage, raw, router, early_y_0, early_y_1, early_z_0, early_z_1, early_total,
     late, late_y, late_sum, late_z, late_all, inverse, weight_in, gain_in,
     load_sem, small_sem, y_send, y_recv, z_send, z_recv, raw_send, raw_recv,
     late_y_send, late_y_recv, late_z_send, late_z_recv, all_send, all_recv,
@@ -39,7 +38,6 @@
     me = lax.axis_index("rows")
     own = lax.axis_index("owner")
     z, y = me // SIDE, lax.rem(me, SIDE)
-    width = PART * LANES
 
     def shifted(step):
         return lax.rem(z + step[0], SIDE) * SIDE + lax.rem(y + step[1], SIDE)
@@ -58,7 +56,7 @@
 
     loads = []
     for matrix, ref, start, tiles in (
-        (0, gate, 0, PART), (0, gate, PART, EARLY - PART), (0, gate, EARLY, TILES - EARLY), (1, up, 0, TILES),
+        *((0, gate, *tiles) for tiles in EAGER), (0, gate, EARLY, TILES - EARLY), (1, up, 0, TILES),
     ):
         here = []
         for g in range(ROWS // GROUP):
@@ -80,6 +78,8 @@
     for d in range(1, OWNERS):
         pl.semaphore_signal(barrier, inc=1, device_id={"owner": lax.rem(own + d, OWNERS)}, device_id_type=MESH)
 
+    early_y, early_z = (early_y_0, early_y_1), (early_z_0, early_z_1)
+
     def squares(matrix, e, tile):
         x = full[matrix, e, :, pl.ds(tile * LANES, LANES)]
         return jnp.sum(x * x, axis=0, keepdims=True)
@@ -90,8 +90,8 @@
 
             @pl.loop(g * GROUP, (g + 1) * GROUP)
             def _(e):
-                for t in range(PART):
-                    early_y[i, y, e, t] = squares(0, e, i * PART + t)
+                for t in range(EAGER[i][1]):
+                    early_y[i][y, e, t] = squares(0, e, EAGER[i][0] + t)
 
     early_squares(0)
     pl.semaphore_wait(barrier, len(NEAR) + OWNERS - 1)
@@ -108,12 +108,12 @@
     def raw_copy(i, half):
         to = shifted(NEAR[i])
         return remote(
-            up.at[to, pl.ds(DEEP - RAW + half * HALF, HALF)], raw.at[i, pl.ds(half * HALF, HALF)],
+            up.at[to, pl.ds(DEEP - RAW + half * HALF, HALF if half == 0 else RAW - HALF)], raw.at[i, pl.ds(half * HALF, HALF if half == 0 else RAW - HALF)],
             raw_send.at[i, half], raw_recv.at[i, half], rows=to,
         )
 
     def early_across(i, slots, at, send, recv, along_z):
-        return across(lambda to: slots.at[i, at], slots.at[i], at, send.at[i], recv.at[i], along_z)
+        return across(lambda to: slots[i].at[at], slots[i], at, send.at[i], recv.at[i], along_z)
 
     def taken(slots):
         return ((slots[0] + slots[1]) + slots[2]) + slots[3]
@@ -132,7 +132,7 @@
                 for t in range(start, TILES):
                     late[lax.rem(e, SIDE), e // SIDE, matrix * TILES + t - EARLY] = squares(matrix, e, t)
 
-    for i in range(1, FIRST):
+    for i in range(1, len(EAGER)):
         early_squares(i)
         y_copies.append(early_across(i, early_y, y, y_send, y_recv, False))
     late_squares(0, EARLY, loads[2])
@@ -145,10 +145,10 @@
     late_y[y] = late[y]
 
     z_copies = []
-    for i in range(FIRST):
+    for i in range(len(EAGER)):
         for copy in y_copies[i]:
             copy.wait_recv()
-        early_z[i, z] = taken(early_y.at[i])
+        early_z[i][z] = taken(early_y[i])
         z_copies.append(early_across(i, early_z, z, z_send, z_recv, True))
         if RAW and i == 0:
             for j in range(len(NEAR)):
@@ -163,55 +163,54 @@
     def early_whole(i):
         for copy in z_copies[i]:
             copy.wait_recv()
-        whole = taken(early_z.at[i])
-        early_total[:, i * PART:(i + 1) * PART] = whole
-        inverse[:, i * PART:(i + 1) * PART] = 1.0 / jnp.sqrt(whole)
-
-    def fill(part, e, deep, write):
-        matrix, start = part // PARTS, lax.rem(part, PARTS) * PART
-        for t in range(PART):
+        whole = taken(early_z[i])
+        start, count = EAGER[i]
+        early_total[:, start:start + count] = whole
+        inverse[:, start:start + count] = 1.0 / jnp.sqrt(whole)
+
+    def fill(message, e, deep, write):
+        matrix, start, count = message
+        for t in range(count):
             columns = pl.ds(pl.multiple_of((start + t) * LANES, LANES), LANES)
-            row = inverse[e, part * PART + t]
+            row = inverse[e, matrix * TILES + start + t]
             value = (full[matrix, e, pl.ds(0, deep), columns] * row).astype(BF16)
-            write(pl.ds(pl.multiple_of(matrix * DEEP, DEEP), deep), columns, value)
-
-    def prepare(step, part, deep):
+            write(pl.ds(matrix * DEEP, deep), columns, value)
+
+    def prepare(step, message, deep):
         to = shifted(step)
 
         def write(rows, columns, value):
             stage[to, rows, columns] = value
 
-        fill(part, to, deep, write)
-
-    def send(step, part, deep):
-        piece = (
-            pl.ds(pl.multiple_of(part // PARTS * DEEP, DEEP), deep),
-            pl.ds(pl.multiple_of(lax.rem(part, PARTS) * width, width), width),
-        )
+        fill(message, to, deep, write)
+
+    def send(step, message, deep):
+        matrix, start, count = message
+        piece = (pl.ds(matrix * DEEP, deep), pl.ds(pl.multiple_of(start * LANES, LANES), count * LANES))
         k = slot(step)
         to = shifted(step)
         remote(
             stage.at[(to, *piece)], land.at[(me, *piece)], data_send.at[k], data_recv.at[k], rows=to
         ).start()
 
-    def batch(part, steps, less=0):
+    def batch(message, less=0):
         waiting = None
-        for step in steps:
+        for step in ORDER:
             deep = DEEP - (less if step in NEAR else 0)
-            prepare(step, part, deep)
+            prepare(step, message, deep)
             if waiting:
-                send(waiting[0], part, waiting[1])
+                send(waiting[0], message, waiting[1])
             waiting = step, deep
-        send(waiting[0], part, waiting[1])
-
-    def for_self(part):
+        send(waiting[0], message, waiting[1])
+
+    def for_self(message):
         def write(rows, columns, value):
             land[me, rows, columns] = value
 
-        fill(part, me, DEEP, write)
+        fill(message, me, DEEP, write)
 
     early_whole(0)
-    batch(0, ORDER)
+    batch((0, *EAGER[0]))
 
     for copy in late_z_copies:
         copy.wait_recv()
@@ -222,13 +221,12 @@
             late_all.at[me], late_all.at[at], all_send.at[slot(step)], all_recv.at[slot(step)], rows=shifted(step)
         )
 
-    for_self(0)
     for step in ORDER:
         all_copy(step, me).start()
 
-    for part in range(1, FIRST):
-        early_whole(part)
-        batch(part, ORDER)
+    for i in range(1, len(EAGER)):
+        early_whole(i)
+        batch((0, *EAGER[i]))
 
     def plane_copy(step, at):
         return remote(
@@ -248,16 +246,14 @@
         all_copy(step, back(step)).wait_recv()
     inverse[:, EARLY:] = 1.0 / jnp.sqrt(late_all[...])
 
-    for part in range(FIRST, PARTS):
-        batch(part, ORDER)
-
-    @pl.loop(PARTS, 2 * PARTS)
+    batch((0, EARLY, TILES - EARLY))
+
+    @pl.loop(0, TILES // PART)
     def _(part):
-        batch(part, ORDER, RAW)
-
-    @pl.loop(1, 2 * PARTS)
-    def _(part):
-        for_self(part)
+        batch((1, part * PART, PART), RAW)
+
+    for_self((0, 0, TILES))
+    for_self((1, 0, TILES))
 
     for step in ORDER:
         plane_copy(step, back(step)).wait_recv()
@@ -343,8 +339,7 @@
             pltpu.VMEM((ROWS, 2 * rows, columns), BF16),
             pltpu.VMEM((len(NEAR), max(RAW, 8), columns), F32),
             pltpu.VMEM((OWNERS, ROWS, LANES // OWNERS, rows), BF16),
-            sums(FIRST, SIDE, experts, PART),
-            sums(FIRST, SIDE, experts, PART),
+            *(sums(SIDE, experts, count) for _, count in EAGER * 2),
             sums(experts, EARLY),
             sums(SIDE, SIDE, LATE),
             sums(SIDE, SIDE, LATE),
@@ -356,7 +351,7 @@
             pltpu.VMEM((1, rows), F32),
             dma((4, ROWS // GROUP)),
             dma((2,)),
-            dma((FIRST, SIDE)), dma((FIRST, SIDE)), dma((FIRST, SIDE)), dma((FIRST, SIDE)),
+            dma((len(EAGER), SIDE)), dma((len(EAGER), SIDE)), dma((len(EAGER), SIDE)), dma((len(EAGER), SIDE)),
             dma((len(NEAR), 2)), dma((len(NEAR), 2)),
             dma((SIDE,)), dma((SIDE,)), dma((SIDE,)), dma((SIDE,)),
             dma((ROWS,)), dma((ROWS,)), dma((ROWS,)), dma((ROWS,)),

time: 89.1 us -> 89.2 us (level)
  no operation moved by 1% of the time
where the time goes in v3:
time: 89.2 us; the launch traced here: 89.1 us
  Pallas kernels  88.5 us (99%)
    pallas_call x1, Pallas kernels, on_device(): pl.pallas_call(exchange, name='exchange', out_shape=(jax.ShapeDtypeStruct...  85.6 us
    pallas_call x1, Pallas kernels, on_device(): pl.pallas_call(lay_out, name='lay_out', out_shape=(ready, ready, router,...  2.91 us

profile of v3, /device:TPU:0, one launch (start us, length us, event | category | flops | bytes accessed | tf_op | source)
XLA Modules:
  0.0 89.1 jit_solution(10964254712174738217)
XLA Ops:
  0.6 85.6 %exchange.1 = (bf16[16,256,768]{2,1,0:T(8,128)(2,1)S(1)}, bf16[2048,128]{1,0:T(8,128)(2,1)S(1)}, f32[1,768]{1,0:T(1,128)S(1)}, f32[1,768]{1,0:T(1,128)S(1)}) custom-call(f32[16,128,768]{2,1,0:T(8,128)} %gate.1, f32[16,128,768]{2,1,0:T(8,128)} %up.1, f32[16,128]{1,0:T(8,128)} %bitcast.4, f32[1,128]{1,0:T(1,128)} %bitcast.5), custom_call_target="tpu_custom_call" | custom-call | tf_op jit(solution)/shard_map/exchange/pallas_call | solution.py:331
  86.2 2.9 %lay_out.1 = (bf16[16,128,768]{2,1,0:T(8,128)(2,1)}, bf16[16,128,768]{2,1,0:T(8,128)(2,1)}, bf16[2048,128]{1,0:T(8,128)(2,1)}, f32[1,768]{1,0:T(1,128)}, f32[1,768]{1,0:T(1,128)}) custom-call(bf16[16,256,768]{2,1,0:T(8,128)(2,1)S(1)} %get-tuple-element.14.land, bf16[2048,128]{1,0:T(8,128)(2,1)S(1)} %get-tuple-element.15.serve, ...), custom_call_target="tpu_custom_call" | custom-call | tf_op jit(solution)/shard_map/lay_out/pallas_call | solution.py:366
